TPU v7x, 16 devices: a whole 2x2x2 slice. The times are simulated.
16 devices in a mesh: col: 2 (over z), row: 8 (over y, x, core).
Axes of the slice: x: 2, y: 2, z: 2, core: 2. Of those that a mesh axis runs over, the one named last changes fastest.
Arguments:
- t_amps: float32 [256, 11664], P('row', 'col')
- denoms: float32 [256, 11664], P('row', 'col')
- v_oovv: bfloat16 [256, 11664], P('row', 'col')
- v_vvvv: bfloat16 [11664, 11664], P('row', 'col')
- v_oooo: bfloat16 [256, 256], replicated
- w_direct: bfloat16 [1728, 1728], P(None, 'col')
- w_exch: bfloat16 [1728, 1728], P(None, 'col')
Outputs:
- output: float32 [256, 11664], P('row', 'col')
All inputs are finite; a program needn't handle non-finite values.
Results may differ from a plain program's by a relative error of at most 0.001.
Values are sent between devices in bfloat16 or wider.
A program may use at most 1 GiB of HBM per device.

v0:
```python
import math
import jax
import jax.numpy as jnp
from jax import lax
from jax.sharding import PartitionSpec as P


def solution(mesh):
    n_row = mesh.shape["row"]
    n_col = mesh.shape["col"]
    amp_spec = P("row", "col")
    wide_spec = P(None, "col")

    def local_sweep(t_blk, d_blk, oovv_blk, vvvv_blk, oooo_full, wd_blk, wx_blk):
        rows_dev, cols_dev = t_blk.shape
        n_occ = math.isqrt(oooo_full.shape[0])
        n_virt = wd_blk.shape[0] // n_occ
        occ_row = n_occ // n_row
        occ_col = n_occ // n_col
        t_half = t_blk.astype(jnp.bfloat16)
        t_rows = lax.all_gather(t_half, "col", axis=1, tiled=True)
        t_ladder = lax.all_to_all(t_rows, "row", 1, 0, tiled=True)
        ladder_part = jnp.dot(t_ladder, vvvv_blk, preferred_element_type=jnp.float32)
        t_cols = lax.all_gather(t_half, "row", axis=0, tiled=True)
        x_part = lax.dot_general(oovv_blk, t_cols, (((1,), (1,)), ((), ())), preferred_element_type=jnp.float32)
        x_rows = lax.psum(x_part, "col")
        row_idx = lax.axis_index("row")
        oooo_rows = lax.dynamic_slice_in_dim(oooo_full, row_idx * rows_dev, rows_dev, axis=0)
        hole_mat = (oooo_rows.astype(jnp.float32) + 0.5 * x_rows).astype(jnp.bfloat16)
        hole_part = lax.dot_general(hole_mat, t_half, (((0,), (0,)), ((), ())), preferred_element_type=jnp.float32)
        ladder_sum = lax.psum_scatter(ladder_part + hole_part, "row", scatter_dimension=0, tiled=True)
        t_four = t_rows.reshape(occ_row, n_occ, n_virt, n_virt)
        direct_term = jnp.einsum("ikac,kcjb->ijab", t_four, wd_blk.reshape(n_occ, n_virt, occ_col, n_virt), preferred_element_type=jnp.float32)
        exch_term = jnp.einsum("ikcb,kcja->ijab", t_four, wx_blk.reshape(n_occ, n_virt, occ_col, n_virt), preferred_element_type=jnp.float32)
        ph_back = lax.all_to_all(direct_term - exch_term, "col", 2, 1, tiled=True)
        swap_row = lax.all_to_all(ph_back, "row", 1, 0, tiled=True)
        swap_both = lax.all_to_all(swap_row, "col", 3, 2, tiled=True)
        ph_sym = (ph_back + swap_both.transpose(1, 0, 3, 2)).reshape(rows_dev, cols_dev)
        residual = oovv_blk.astype(jnp.float32) + ladder_sum + ph_sym
        return residual / d_blk

    return jax.shard_map(local_sweep, mesh=mesh, in_specs=(amp_spec, amp_spec, amp_spec, amp_spec, P(), wide_spec, wide_spec), out_specs=amp_spec, check_vma=False)
```

profile of v0, /device:TPU:0, one launch (start us, length us, event | category | flops | bytes accessed | tf_op | source)
XLA Modules:
  0.0 175.1 jit_solution(4487887738798408607)
XLA Ops:
  6.5 1.9 %convert_element_type.13 = bf16[32,5832]{1,0:T(8,128)(2,1)} convert(f32[32,5832]{1,0:T(8,128)} %param.7) | non-fusion elementwise | flops 186624 | bytes 1119744 | tf_op jit(solution)/shard_map/convert_element_type | solution.py:20
  9.6 12.7 %all-gather = bf16[2,5832,32]{1,2,0:T(8,128)(2,1)S(1)} all-gather(bf16[1,5832,32]{1,2,0:T(8,128)(2,1)S(1)} %convert_bitcast_fusion), channel_id=1, replica_groups=mesh['col'=2,'row'=8] {'col'}, dimensions={0}, use_global_device_ids=true | all-gather | bytes 1119744 | tf_op jit(solution)/shard_map/all_gather | solution.py:21
  26.4 3.9 %all-to-all-start = ((bf16[32,8,1458]{2,0,1:T(8,128)(2,1)}), bf16[32,8,1458]{2,0,1:T(8,128)(2,1)S(1)}, u32[]{:S(2)}, u32[]{:S(2)}) async-start(bf16[32,8,1458]{2,0,1:T(8,128)(2,1)} %copy.46), calls=%async_computation | async-start | bytes 1572864 | tf_op jit(solution)/shard_map/all_to_all | solution.py:22
  30.3 17.4 %all-to-all-done = bf16[32,8,1458]{2,0,1:T(8,128)(2,1)S(1)} async-done(((bf16[32,8,1458]{2,0,1:T(8,128)(2,1)}), bf16[32,8,1458]{2,0,1:T(8,128)(2,1)S(1)}, u32[]{:S(2)}, u32[]{:S(2)}) %all-to-all-start) | async-done | bytes 746528 | tf_op jit(solution)/shard_map/all_to_all | solution.py:22
  47.7 11.3 %fusion.17 = f32[256,5832]{1,0:T(8,128)} fusion(bf16[256,1458]{1,0:T(8,128)(2,1)S(1)} %bitcast.65, bf16[1458,5832]{1,0:T(8,128)(2,1)} %param.10), kind=kOutput, calls=%fused_computation.17 | convolution fusion | flops 4353564672 | bytes 23724576 | tf_op jit(solution)/shard_map/dot_general | solution.py:23
  59.0 2.9 %fusion.18 = f32[32,256]{1,0:T(8,128)S(1)} fusion(bf16[32,5832]{1,0:T(8,128)(2,1)S(1)} %copy-done.1, bf16[256,5832]{1,0:T(8,128)(2,1)} %all-gather.3.cloned.1.call-done), kind=kOutput, calls=%fused_computation.18 | convolution fusion | flops 95551488 | bytes 3392000 | tf_op jit(solution)/shard_map/dot_general | solution.py:25
  61.8 8.5 %psum.7 = f32[32,256]{1,0:T(8,128)S(1)} all-reduce(f32[32,256]{1,0:T(8,128)S(1)} %fusion.18), channel_id=1, replica_groups=mesh['col'=2,'row'=8] {'col'}, use_global_device_ids=true, to_apply=%region_0.0 | all-reduce | flops 8192 | bytes 65536 | tf_op jit(solution)/shard_map/psum | solution.py:26
  70.4 6.3 %convolution_add_fusion = f32[256,5832]{1,0:T(8,128)} fusion(f32[256,5832]{1,0:T(8,128)} %fusion.17, bf16[32,5832]{1,0:T(8,128)(2,1)S(1)} %copy-done, f32[32,256]{1,0:T(8,128)S(1)} %psum.7, bf16[256,256]{1,0:T(8,128)(2,1)} %param.11, s32[]{:T(128)S(6)} %select_n.3), kind=kOutput, calls=%fused_computation | convolution fusion | flops 97077248 | bytes 12423684 | tf_op jit(solution)/shard_map/dot_general | solution.py:30
  76.7 2.8 %reshape.22 = bf16[2,16,108,108,1]{3,2,1,0,4:T(8,128)(2,1)} reshape(bf16[32,11664]{1,0:T(8,128)(2,1)S(1)} %bitcast.59) | data formatting | bytes 1492992 | tf_op jit(solution)/shard_map/reshape | solution.py:32
  79.5 7.5 %reshape.15 = bf16[16,108,8,108]{3,2,1,0:T(8,128)(2,1)} reshape(bf16[1728,864]{1,0:T(8,128)(2,1)} %param.12) | data formatting | bytes 5971968 | tf_op jit(solution)/shard_map/reshape | solution.py:33
  87.1 6.4 %reshape.17 = bf16[16,108,8,108]{3,2,1,0:T(8,128)(2,1)S(1)} reshape(bf16[1728,864]{1,0:T(8,128)(2,1)} %param.13) | data formatting | bytes 5971968 | tf_op jit(solution)/shard_map/reshape | solution.py:34
  93.5 3.5 %fusion.4 = f32[2,8,108,108]{2,3,0,1:T(8,128)S(1)} fusion(bf16[2,16,108,108,1]{3,2,1,0,4:T(8,128)(2,1)} %reshape.22, bf16[16,108,8,108,1]{3,2,1,0,4:T(8,128)(2,1)} %bitcast.61), kind=kOutput, calls=%fused_computation.6 | convolution fusion | flops 644972544 | bytes 4478976 | tf_op jit(solution)/shard_map/ikac,kcjb->ijab/dot_general | solution.py:33
  97.0 2.0 %fusion.10 = f32[2,8,108,108]{2,3,0,1:T(8,128)} fusion(f32[2,8,108,108]{2,3,0,1:T(8,128)S(1)} %fusion.4, bf16[2,16,108,108,1]{3,2,1,0,4:T(8,128)(2,1)S(1)} %copy-done.3, bf16[16,108,8,108,1]{3,2,1,0,4:T(8,128)(2,1)S(1)} %bitcast.60), kind=kOutput, calls=%fused_computation.8 | convolution fusion | flops 645159168 | bytes 5225472 | tf_op jit(solution)/shard_map/ikcb,kcja->ijab/dot_general | solution.py:34
  99.0 1.7 copy.50
  100.6 10.9 %all_to_all.73 = f32[2,8,108,108]{3,1,0,2:T(8,128)S(1)} all-to-all(f32[2,8,108,108]{3,1,0,2:T(8,128)S(1)} %copy.50), channel_id=1, replica_groups=mesh['col'=2,'row'=8] {'col'}, dimensions={2} | all-to-all | bytes 1492992 | tf_op jit(solution)/shard_map/all_to_all | solution.py:35
  112.3 24.4 %all_to_all.74 = f32[2,16,54,108]{3,0,2,1:T(2,128)S(1)} all-to-all(f32[2,16,54,108]{3,0,2,1:T(2,128)S(1)} %copy.53), channel_id=1, replica_groups=mesh['col'=2,'row'=8] {'row'}, dimensions={1} | all-to-all | bytes 1492992 | tf_op jit(solution)/shard_map/all_to_all | solution.py:36
  137.1 1.7 copy.55
  138.8 2.3 %reshape.27 = f32[2,1,93312]{2,1,0:T(1,128)S(1)} reshape(f32[108,2,16,54]{3,2,1,0:T(8,128)S(1)} %bitcast.57) | data formatting | bytes 1492992
  141.0 12.6 %all_to_all.75 = f32[2,1,93312]{2,1,0:T(1,128)S(1)} all-to-all(f32[2,1,93312]{2,1,0:T(1,128)S(1)} %reshape.27), channel_id=1, replica_groups=mesh['col'=2,'row'=8] {'col'}, dimensions={0} | all-to-all | bytes 1492992 | tf_op jit(solution)/shard_map/all_to_all | solution.py:37
  154.2 3.0 %reduce = f32[2,93312]{1,0:T(2,128)S(1)} reduce(f32[2,1,93312]{2,1,0:T(1,128)S(1)} %all_to_all.75, f32[]{:T(128)} %broadcast), dimensions={1}, to_apply=%all_to_all.65.reduce_sub_computation | reduce | bytes 1492996 | tf_op jit(solution)/shard_map/all_to_all | solution.py:37
  157.2 2.7 %reshape.28 = f32[108,2,16,54]{3,2,1,0:T(8,128)S(1)} reshape(f32[2,93312]{1,0:T(2,128)S(1)} %reduce) | data formatting | bytes 1492992
  159.9 2.6 %copy.85 = f32[16,2,54,2,54]{2,3,0,4,1:T(2,128)} copy(f32[16,2,54,2,54]{2,0,1,4,3:T(8,128)S(1)} %bitcast.55) | data formatting | bytes 1492992 | tf_op jit(solution)/shard_map/all_to_all | solution.py:37
  162.5 2.4 %all_to_all.68 = f32[16,2,108,54]{2,0,3,1:T(8,128)S(1)} reshape(f32[16,2,2,54,54]{3,2,0,4,1:T(2,128)} %bitcast.56) | data formatting | bytes 1492992 | tf_op jit(solution)/shard_map/all_to_all | solution.py:37
  166.2 2.1 %add_divide_fusion = f32[32,5832]{1,0:T(8,128)} fusion(f32[32,5832]{1,0:T(8,128)S(1)} %copy-done.4, f32[32,5832]{1,0:T(8,128)S(1)} %reshape.18, f32[32,5832]{1,0:T(8,128)} %reduce-scatter.2.cloned.1.call-done, bf16[32,5832]{1,0:T(8,128)(2,1)S(1)} %copy-done.2), kind=kLoop, calls=%fused_computation.11 | loop fusion | flops 746496 | bytes 3359232 | tf_op jit(solution)/shard_map/div | solution.py:40
  (28 shorter events, 8.0 us)
Async XLA Ops:
  6.5 52.4 %all-gather.3.cloned.1.call-start = ((), (), s32[]{:S(2)}) async-start(), calls=%async_computation.5 | async-start | bytes 3391488 | tf_op jit(solution)/shard_map/all_gather | solution.py:24
  26.4 21.3 %all-to-all-start = ((bf16[32,8,1458]{2,0,1:T(8,128)(2,1)}), bf16[32,8,1458]{2,0,1:T(8,128)(2,1)S(1)}, u32[]{:S(2)}, u32[]{:S(2)}) async-start(bf16[32,8,1458]{2,0,1:T(8,128)(2,1)} %copy.46), calls=%async_computation | async-start | bytes 1572864 | tf_op jit(solution)/shard_map/all_to_all | solution.py:22
  30.2 135.4 %reduce-scatter.2.cloned.1.call-start = ((), (), s32[]{:S(2)}) async-start(), calls=%async_computation.6 | async-start | bytes 6782976 | tf_op jit(solution)/shard_map/reduce_scatter | solution.py:31
  47.6 11.3 %copy-start.1 = (bf16[32,5832]{1,0:T(8,128)(2,1)S(1)}, bf16[32,5832]{1,0:T(8,128)(2,1)}, u32[]{:S(2)}) copy-start(bf16[32,5832]{1,0:T(8,128)(2,1)} %param.9) | copy-start | bytes 1119748
  59.0 11.4 %copy-start = (bf16[32,5832]{1,0:T(8,128)(2,1)S(1)}, bf16[32,5832]{1,0:T(8,128)(2,1)}, u32[]{:S(2)}) copy-start(bf16[32,5832]{1,0:T(8,128)(2,1)} %convert_element_type.13) | copy-start | bytes 1119748
  93.5 3.5 %copy-start.3 = (bf16[2,16,108,108,1]{3,2,1,0,4:T(8,128)(2,1)S(1)}, bf16[2,16,108,108,1]{3,2,1,0,4:T(8,128)(2,1)}, u32[]{:S(2)}) copy-start(bf16[2,16,108,108,1]{3,2,1,0,4:T(8,128)(2,1)} %reshape.22) | copy-start | bytes 2239492
  164.9 1.0 copy-start.2
  165.0 1.2 copy-start.4
Sparse Core Ops, SparseCore 0:
  9.2 36.7 all-gather.2
  76.8 60.1 reduce-scatter.1
where the time goes:
time: 176 us; the launch traced here: 175 us
  blocking collectives  69.2 us (39%)
  local copies, waits for them, and re-layouts  36.8 us (21%)
  matrix products  25.9 us (15%)
  waiting for transfers between devices  17.4 us (10%)
  between operations  13.6 us (8%)
  other arithmetic  8.27 us (5%)
  starting transfers between devices  3.92 us (2%)
    all_to_all x1, blocking collectives, local_sweep(): swap_row = lax.all_to_all(ph_back, 'row', 1, 0, tiled=True)  24.4 us
    all_to_all x1, waiting for transfers between devices, local_sweep(): t_ladder = lax.all_to_all(t_rows, 'row', 1, 0, tiled=True)  17.4 us
    all_gather x1, blocking collectives, local_sweep(): t_rows = lax.all_gather(t_half, 'col', axis=1, tiled=True)  12.7 us
    all_to_all x1, blocking collectives, local_sweep(): swap_both = lax.all_to_all(swap_row, 'col', 3, 2, tiled=True)  12.6 us
    dot_general x1, matrix products, local_sweep(): jnp.dot(t_ladder, vvvv_blk, preferred_element_type=jnp.float32)  11.3 us
    all_to_all x1, blocking collectives, local_sweep(): ph_back = lax.all_to_all(direct_term - exch_term, 'col', 2, 1, tiled=True)  10.9 us
    psum x1, blocking collectives, local_sweep(): x_rows = lax.psum(x_part, 'col')  8.53 us
    reshape x1, local copies, waits for them, and re-layouts, local_sweep(): wd_blk.reshape(n_occ, n_virt, occ_col, n_virt)  7.55 us
  transfers between devices with their start and end apart: 3, of which 1 were waited for; matrix products, arithmetic and copies ran while one was open for 30% of the time, Pallas kernels for 0%

commit v1 on v0

v1 whole, which is shorter than its diff:
```python
import functools
import jax
import jax.numpy as jnp
from jax import lax
from jax.experimental import pallas as pl
from jax.experimental.pallas import tpu as pltpu
from jax.sharding import PartitionSpec as P

F32 = jnp.float32
BF16 = jnp.bfloat16
OCC = 16
VIRT = 108
NR = 8
HALF = VIRT // 2
CBLK = VIRT * VIRT // NR
COLS = VIRT * VIRT // 2
ROWS = 2 * OCC
CW = 768
NCH = -(-COLS // CW)
LASTW = COLS - (NCH - 1) * CW
HP = 56
VP = 112
VM = pl.BlockSpec(memory_space=pltpu.VMEM)
ANY = pl.BlockSpec(memory_space=pl.ANY)
MESH = pl.DeviceIdType.MESH


def nt_dot(a, b):
    return lax.dot_general(a, b, (((1,), (1,)), ((), ())), preferred_element_type=F32)


def rcopy(src, dst, ssem, rsem, row, col):
    return pltpu.make_async_remote_copy(src_ref=src, dst_ref=dst, send_sem=ssem, recv_sem=rsem,
                                        device_id={"row": row, "col": col}, device_id_type=MESH)


def greet(barrier, row, col):
    pl.semaphore_signal(barrier, inc=1, device_id={"row": row, "col": col}, device_id_type=MESH)


def gather_kernel(t_ref, v_ref, oo_ref, lad, tf, tb, mt, vs, vl, xp, xr, mm,
                  z_s, z_r, l_s, l_r, v_s, v_r, x_s, x_r, m_s, m_r):
    r = lax.axis_index("row")
    c = lax.axis_index("col")
    oc = 1 - c
    barrier = pltpu.get_barrier_semaphore()
    for d in range(1, NR):
        rp = lax.rem(r + d, NR)
        greet(barrier, rp, c)
        greet(barrier, rp, oc)
    greet(barrier, r, oc)

    tb[...] = t_ref[...].astype(BF16)
    for m in range(4):
        tf[4 * c + m] = t_ref[:, m * CBLK:(m + 1) * CBLK].astype(BF16)
        vs[m] = v_ref[:, m * CBLK:(m + 1) * CBLK]
    pl.semaphore_wait(barrier, 2 * NR - 1)

    zc = [rcopy(tf.at[4 * c + m], tf.at[4 * c + m], z_s.at[m], z_r.at[m], r, oc) for m in range(4)]
    for cp in zc:
        cp.start()

    def ladder(rp):
        return rcopy(tf.at[rp], lad.at[r], l_s.at[rp], l_r.at[r], rp, c)

    def send_ladder(rp):
        @pl.when(rp != r)
        def _():
            ladder(rp).start()

        @pl.when(rp == r)
        def _():
            lad[r] = tf[rp]

    for m in range(4):
        send_ladder(4 * c + m)

    def vcopy(m, cp):
        return rcopy(vs.at[m, pl.ds(16 * cp, 16)], vl.at[r], v_s.at[m, cp], v_r.at[r], 4 * c + m, cp)

    for m in range(4):
        for cp in range(2):
            self = jnp.logical_and(4 * c + m == r, c == cp)

            @pl.when(jnp.logical_not(self))
            def _():
                vcopy(m, cp).start()

            @pl.when(self)
            def _():
                vl[r] = vs[m, 16 * cp:16 * cp + 16]

    for m in range(4):
        rcopy(tf.at[4 * oc + m], tf.at[4 * oc + m], z_s.at[m], z_r.at[m], r, oc).wait_recv()
        send_ladder(4 * oc + m)

    for d in range(1, NR):
        s = lax.rem(r + d, NR)
        rcopy(lad.at[s], lad.at[s], l_s.at[s], l_r.at[s], s, c).wait_recv()
    for s in range(NR):
        @pl.when(jnp.logical_not(jnp.logical_and(s == r, c == s // 4)))
        def _():
            rcopy(vl.at[s], vl.at[s], v_s.at[0, 0], v_r.at[s], s, c).wait_recv()

    xp[...] = nt_dot(vl[...].reshape(NR * 16, CBLK), lad[...].reshape(NR * ROWS, CBLK)).reshape(NR, 16, NR * ROWS)

    def xcopy(s):
        return rcopy(xp.at[s], xr.at[r], x_s.at[s], x_r.at[r], s, c)

    for d in range(1, NR):
        xcopy(lax.rem(r + d, NR)).start()
    xr[r] = xp[r]
    for d in range(1, NR):
        s = lax.rem(r + d, NR)
        rcopy(xr.at[s], xr.at[s], x_s.at[s], x_r.at[s], s, c).wait_recv()
    xsum = xr[0]
    for s in range(1, NR):
        xsum = xsum + xr[s]
    oo = oo_ref[pl.ds(pl.multiple_of(ROWS * r + 16 * c, 16), 16), :]
    mm[c] = (oo.astype(F32) + 0.5 * xsum).astype(BF16)
    mcp = rcopy(mm.at[c], mm.at[c], m_s, m_r, r, oc)
    mcp.start()
    rcopy(mm.at[oc], mm.at[oc], m_s, m_r, r, oc).wait_recv()
    mt[...] = mm[...].reshape(ROWS, NR * ROWS).astype(F32).T.astype(BF16)

    mcp.wait_send()
    for cp in zc:
        cp.wait_send()
    for d in range(1, NR):
        s = lax.rem(r + d, NR)
        ladder(s).wait_send()
        xcopy(s).wait_send()
    for m in range(4):
        for cp in range(2):
            @pl.when(jnp.logical_not(jnp.logical_and(4 * c + m == r, c == cp)))
            def _():
                vcopy(m, cp).wait_send()


def gather_call(t_blk, v_blk, oooo):
    dma = pltpu.SemaphoreType.DMA
    return pl.pallas_call(
        gather_kernel,
        name="gather",
        out_shape=(
            jax.ShapeDtypeStruct((NR, ROWS, CBLK), BF16),
            jax.ShapeDtypeStruct((NR, ROWS, CBLK), BF16),
            jax.ShapeDtypeStruct((ROWS, COLS), BF16),
            jax.ShapeDtypeStruct((NR * ROWS, ROWS), BF16),
        ),
        in_specs=[VM] * 3,
        out_specs=(VM,) * 4,
        scratch_shapes=[
            pltpu.VMEM((4, ROWS, CBLK), BF16),
            pltpu.VMEM((NR, 16, CBLK), BF16),
            pltpu.VMEM((NR, 16, NR * ROWS), F32),
            pltpu.VMEM((NR, 16, NR * ROWS), F32),
            pltpu.VMEM((2, 16, NR * ROWS), BF16),
            dma((4,)), dma((4,)), dma((NR,)), dma((NR,)), dma((4, 2)), dma((NR,)),
            dma((NR,)), dma((NR,)), dma, dma,
        ],
        compiler_params=pltpu.CompilerParams(collective_id=0, has_side_effects=True),
        cost_estimate=pl.CostEstimate(flops=2 * 128 * 256 * CBLK, bytes_accessed=4 * 10**6, transcendentals=0),
    )(t_blk, v_blk, oooo)


def ph_kernel(tf, wd, wx, so, sto, rr, td, te, dd, ff):
    for a in range(VIRT):
        p = a * VIRT
        b, off = p // CBLK, p % CBLK
        n1 = min(VIRT, CBLK - off)
        rr[a * ROWS:(a + 1) * ROWS, 0:n1] = tf[b, :, off:off + n1].astype(F32)
        if n1 < VIRT:
            rr[a * ROWS:(a + 1) * ROWS, n1:VIRT] = tf[b + 1, :, 0:VIRT - n1].astype(F32)
    for i in range(2):
        for k in range(OCC):
            blk = rr[pl.ds(i * OCC + k, 128, stride=ROWS), :]
            td[i * VP:i * VP + VIRT, k * VIRT:(k + 1) * VIRT] = blk[:VIRT, :VIRT].astype(BF16)
            te[i * VP:i * VP + VIRT, k * VIRT:(k + 1) * VIRT] = blk.T[:VIRT, :VIRT].astype(BF16)
    dd[...] = jnp.dot(td[...], wd[...], preferred_element_type=F32)
    ff[...] = jnp.dot(te[...], wx[...], preferred_element_type=F32)
    for j in range(OCC // 2):
        for i in range(2):
            d_ij = dd[i * VP:i * VP + VP, j * VIRT:(j + 1) * VIRT]
            f_ij = ff[i * VP:i * VP + VP, j * VIRT:(j + 1) * VIRT]
            s = d_ij[:VIRT, :VIRT] - f_ij.T[:VIRT, :VIRT]
            st = d_ij.T[:VIRT, :VIRT] - f_ij[:VIRT, :VIRT]
            for h in range(2):
                so[h, j, i, 0:HALF, 0:VIRT] = s[h * HALF:(h + 1) * HALF]
                sto[h, j // 2, 2 * (j % 2) + i, 0:HALF, 0:VIRT] = st[h * HALF:(h + 1) * HALF]


def ph_call(tf, wd, wx):
    ncol = wd.shape[1]
    return pl.pallas_call(
        ph_kernel,
        name="ph",
        out_shape=(
            jax.ShapeDtypeStruct((2, 8, 2, HP, 128), F32),
            jax.ShapeDtypeStruct((2, 4, 4, HP, 128), F32),
        ),
        in_specs=[VM] * 3,
        out_specs=(VM,) * 2,
        scratch_shapes=[
            pltpu.VMEM((128 * ROWS, 128), F32),
            pltpu.VMEM((2 * VP, OCC * VIRT), BF16),
            pltpu.VMEM((2 * VP, OCC * VIRT), BF16),
            pltpu.VMEM((2 * VP, ncol), F32),
            pltpu.VMEM((2 * VP, ncol), F32),
        ],
        cost_estimate=pl.CostEstimate(flops=4 * 224 * 1728 * 864, bytes_accessed=8 * 10**6, transcendentals=0),
    )(tf, wd, wx)


def ladder_kernel(lad, mt, tb, so, sto, v_hbm, rs, sz, strr, vbuf, part, d2d, r1, r2, stz,
                  v_sem, d_s, d_r, a_s, a_r, b_s, b_r, s_s, s_r, t_s, t_r):
    row = lax.axis_index("row")
    c = lax.axis_index("col")
    oc = 1 - c
    core = lax.rem(row, 2)
    q = row // 2
    x, y = lax.rem(q, 2), q // 2
    qs = {"x": 2 * y + 1 - x, "y": 2 * (1 - y) + x, "d": 2 * (1 - y) + 1 - x}
    barrier = pltpu.get_barrier_semaphore()
    for d in range(1, NR):
        greet(barrier, lax.rem(row + d, NR), c)
    greet(barrier, row, oc)

    v_copy = pltpu.make_async_copy(v_hbm, vbuf, v_sem)
    v_copy.start()
    pl.semaphore_wait(barrier, NR)

    stz_cp = rcopy(sto.at[oc], stz, s_s.at[0], s_r.at[0], row, oc)
    sz_cp = rcopy(so.at[oc], sz, s_s.at[1], s_r.at[1], row, oc)
    stz_cp.start()
    sz_cp.start()

    def tcopy(jr, own):
        rp = 4 * c + jr if own else 4 * oc + jr
        src = sto.at[c, jr] if own else stz.at[jr]
        return rp, rcopy(src, strr.at[row], t_s.at[rp], t_r.at[row], rp, c)

    def send_t(jr, own):
        rp, cp = tcopy(jr, own)

        @pl.when(rp != row)
        def _():
            cp.start()

        @pl.when(rp == row)
        def _():
            strr[row] = sto[c, jr] if own else stz[jr]

    for jr in range(4):
        send_t(jr, True)

    def d_copy(n):
        return rcopy(part.at[n, :, 1 - core], d2d.at[n], d_s.at[n], d_r.at[n], 2 * q + 1 - core, c)

    XR = pl.ds(0, 16)
    YR = pl.ds(16, 16)

    def a_copies(n):
        out = []
        for e, (nb, far, rows) in enumerate((("x", "x", XR), ("x", "d", XR), ("y", "y", YR), ("y", "d", YR))):
            out.append(rcopy(part.at[n, qs[far], core, rows], r1.at[n, e], a_s.at[n, e], a_r.at[n, e],
                             2 * qs[nb] + core, c))
        return out

    def b_copies(n):
        return [rcopy(part.at[n, qs["y"], core, XR], r2.at[n, 0], b_s.at[n, 0], b_r.at[n, 0], 2 * qs["y"] + core, c),
                rcopy(part.at[n, qs["x"], core, YR], r2.at[n, 1], b_s.at[n, 1], b_r.at[n, 1], 2 * qs["x"] + core, c)]

    def compute(n):
        w = CW if n < NCH - 1 else LASTW
        p = jnp.dot(lad[...], vbuf[:, n * CW:n * CW + w], preferred_element_type=F32)
        p = p + jnp.dot(mt[...], tb[:, n * CW:n * CW + w], preferred_element_type=F32)
        part[n, :, :, :, 0:w] = p.reshape(4, 2, ROWS, w)
        d_copy(n).start()

    def first(n):
        d_copy(n).wait_recv()
        for k in range(4):
            part[n, k, core] = part[n, k, core] + d2d[n, k]
        for cp in a_copies(n):
            cp.start()

    v_copy.wait()
    for n in range(NCH):
        compute(n)
        if n >= 1:
            first(n - 1)
    first(NCH - 1)

    rcopy(stz, stz, s_s.at[0], s_r.at[0], row, oc).wait_recv()
    for jr in range(4):
        send_t(jr, False)

    def second(n):
        for cp in a_copies(n):
            cp.wait_recv()
        part[n, qs["y"], core, 0:16] = part[n, qs["y"], core, 0:16] + r1[n, 1]
        part[n, qs["x"], core, 16:32] = part[n, qs["x"], core, 16:32] + r1[n, 3]
        for cp in b_copies(n):
            cp.start()

    for n in range(NCH):
        second(n)

    def third(n):
        for cp in b_copies(n):
            cp.wait_recv()
        rs[n, 0:16] = part[n, q, core, 0:16] + r1[n, 0] + r2[n, 0]
        rs[n, 16:32] = part[n, q, core, 16:32] + r1[n, 2] + r2[n, 1]

    for n in range(NCH):
        third(n)

    rcopy(sz, sz, s_s.at[1], s_r.at[1], row, oc).wait_recv()
    for d in range(1, NR):
        s = lax.rem(row + d, NR)
        rcopy(strr.at[s], strr.at[s], t_s.at[s], t_r.at[s], s, c).wait_recv()
    stz_cp.wait_send()
    sz_cp.wait_send()
    for d in range(1, NR):
        s = lax.rem(row + d, NR)
        rcopy(strr.at[s], strr.at[s], t_s.at[s], t_r.at[s], s, c).wait_send()
    for n in range(NCH):
        d_copy(n).wait_send()
        for cp in a_copies(n) + b_copies(n):
            cp.wait_send()


def ladder_call(lad, mt, tb, so, sto, vvvv):
    dma = pltpu.SemaphoreType.DMA
    return pl.pallas_call(
        ladder_kernel,
        name="ladder",
        out_shape=(
            jax.ShapeDtypeStruct((NCH, ROWS, CW), F32),
            jax.ShapeDtypeStruct((8, 2, HP, 128), F32),
            jax.ShapeDtypeStruct((NR, 4, HP, 128), F32),
        ),
        in_specs=[VM] * 5 + [ANY],
        out_specs=(VM,) * 3,
        scratch_shapes=[
            pltpu.VMEM((CBLK, COLS), BF16),
            pltpu.VMEM((NCH, 4, 2, ROWS, CW), F32),
            pltpu.VMEM((NCH, 4, ROWS, CW), F32),
            pltpu.VMEM((NCH, 4, 16, CW), F32),
            pltpu.VMEM((NCH, 2, 16, CW), F32),
            pltpu.VMEM((4, 4, HP, 128), F32),
            dma, dma((NCH,)), dma((NCH,)), dma((NCH, 4)), dma((NCH, 4)), dma((NCH, 2)), dma((NCH, 2)),
            dma((2,)), dma((2,)), dma((NR,)), dma((NR,)),
        ],
        compiler_params=pltpu.CompilerParams(collective_id=1, has_side_effects=True, vmem_limit_bytes=60 * 2**20),
        cost_estimate=pl.CostEstimate(flops=2 * 256 * CBLK * COLS, bytes_accessed=20 * 10**6, transcendentals=0),
    )(lad, mt, tb, so, sto, vvvv)


def final_kernel(rs, v_ref, d_ref, so, sz, strr, out, rr, zz):
    c = lax.axis_index("col")
    oc = 1 - c
    for i in range(2):
        for jj in range(8):
            for mine in range(2):
                h = c if mine else oc
                blk = so[c, jj, i, 0:HALF] if mine else sz[jj, i, 0:HALF]
                blk = blk + strr[4 * h + jj // 2, 2 * i + jj % 2, 0:HALF]
                rr[pl.ds(i * OCC + 8 * h + jj, HALF, stride=ROWS), :] = blk
    for a in range(HALF):
        zz[:, a * VIRT:(a + 1) * VIRT] = rr[a * ROWS:(a + 1) * ROWS, 0:VIRT]
    for n in range(NCH):
        w = CW if n < NCH - 1 else LASTW
        sl = slice(n * CW, n * CW + w)
        out[:, sl] = (v_ref[:, sl].astype(F32) + rs[n, :, 0:w] + zz[:, sl]) / d_ref[:, sl]


def final_call(rs, v_blk, d_blk, so, sz, strr):
    return pl.pallas_call(
        final_kernel,
        name="final",
        out_shape=jax.ShapeDtypeStruct((ROWS, COLS), F32),
        in_specs=[VM] * 6,
        out_specs=VM,
        scratch_shapes=[pltpu.VMEM((HALF * ROWS, 128), F32), pltpu.VMEM((ROWS, COLS), F32)],
        cost_estimate=pl.CostEstimate(flops=10**6, bytes_accessed=4 * 10**6, transcendentals=0),
    )(rs, v_blk, d_blk, so, sz, strr)


def solution(mesh):
    amp_spec = P("row", "col")
    wide_spec = P(None, "col")

    def local_sweep(t_blk, d_blk, oovv_blk, vvvv_blk, oooo_full, wd_blk, wx_blk):
        lad, tf, tb, mt = gather_call(t_blk, oovv_blk, oooo_full)
        so, sto = ph_call(tf, wd_blk, wx_blk)
        rs, sz, strr = ladder_call(lad.reshape(NR * ROWS, CBLK), mt, tb, so, sto, vvvv_blk)
        return final_call(rs, oovv_blk, d_blk, so, sz, strr)

    return jax.shard_map(local_sweep, mesh=mesh, in_specs=(amp_spec, amp_spec, amp_spec, amp_spec, P(), wide_spec, wide_spec), out_specs=amp_spec, check_vma=False)
```

time: 176 us -> 97.6 us (0.55)
  Pallas kernels: 0 us -> 97.4 us
  blocking collectives: 69.2 us -> 0 us
  local copies, waits for them, and re-layouts: 36.8 us -> 0 us
  matrix products: 25.9 us -> 0 us
  waiting for transfers between devices: 17.4 us -> 0 us
  between operations: 13.6 us -> 0.02 us
  other arithmetic: 8.27 us -> 0 us
  starting transfers between devices: 3.92 us -> 0 us
    pallas_call x0 -> x4, Pallas kernels: none -> 97.4 us  [the longest x1 48.9 us: ladder_call(): pl.pallas_call(ladder_kernel, name='ladder', out_shape=(jax.ShapeDtypeStr...]
    all_to_all x3 -> x0, blocking collectives: 48 us -> none  [the longest x1 24.4 us: local_sweep(): swap_row = lax.all_to_all(ph_back, 'row', 1, 0, tiled=True)]
    dot_general x5 -> x0, matrix products: 25.9 us -> none  [the longest x1 11.3 us: local_sweep(): jnp.dot(t_ladder, vvvv_blk, preferred_element_type=jnp.float32)]
    all_to_all x1 -> x0, waiting for transfers between devices: 17.4 us -> none  [local_sweep(): t_ladder = lax.all_to_all(t_rows, 'row', 1, 0, tiled=True)]
    reshape x4 -> x0, local copies, waits for them, and re-layouts: 17.1 us -> none  [the longest x1 7.55 us: local_sweep(): wd_blk.reshape(n_occ, n_virt, occ_col, n_virt)]
    all_gather x1 -> x0, blocking collectives: 12.7 us -> none  [local_sweep(): t_rows = lax.all_gather(t_half, 'col', axis=1, tiled=True)]
    all_to_all x9 -> x0, local copies, waits for them, and re-layouts: 10.9 us -> none  [the longest x3 5.52 us: local_sweep(): swap_both = lax.all_to_all(swap_row, 'col', 3, 2, tiled=True)]
    psum x1 -> x0, blocking collectives: 8.53 us -> none  [local_sweep(): x_rows = lax.psum(x_part, 'col')]
  transfers between devices with their start and end apart: 3 -> 0, of which waited for: 1 -> 0; matrix products, arithmetic and copies ran while one was open for 30% -> 0% of each run, Pallas kernels for 0% -> 0%
where the time goes in v1:
time: 97.6 us; the launch traced here: 97.4 us
  Pallas kernels  97.4 us (100%)
    pallas_call x1, Pallas kernels, ladder_call(): pl.pallas_call(ladder_kernel, name='ladder', out_shape=(jax.ShapeDtypeStr...  48.9 us
    pallas_call x1, Pallas kernels, gather_call(): pl.pallas_call(gather_kernel, name='gather', out_shape=(jax.ShapeDtypeStr...  32.5 us
    pallas_call x1, Pallas kernels, ph_call(): pl.pallas_call(ph_kernel, name='ph', out_shape=(jax.ShapeDtypeStruct((2,...  12 us
    pallas_call x1, Pallas kernels, final_call(): pl.pallas_call(final_kernel, name='final', out_shape=jax.ShapeDtypeStruct...  3.98 us

profile of v1, /device:TPU:0, one launch (start us, length us, event | category | flops | bytes accessed | tf_op | source)
XLA Modules:
  0.0 97.4 jit_solution(15267662594785770286)
XLA Ops:
  0.0 32.5 %gather.1 = (bf16[8,32,1458]{2,1,0:T(8,128)(2,1)}, bf16[8,32,1458]{2,1,0:T(8,128)(2,1)}, bf16[32,5832]{1,0:T(8,128)(2,1)}, bf16[256,32]{1,0:T(8,128)(2,1)}) custom-call(f32[32,5832]{1,0:T(8,128)} %t_ref.1, bf16[32,5832]{1,0:T(8,128)(2,1)} %v_ref.3, bf16[256,256]{1,0:T(8,128)(2,1)} %oo_ref.1), custom_call_target="tpu_custom_call" | custom-call | flops 95551488 | bytes 4000000 | tf_op jit(solution)/shard_map/gather/pallas_call | solution.py:142
  32.5 12.0 %ph.1 = (f32[2,8,2,56,128]{4,3,2,1,0:T(8,128)}, f32[2,4,4,56,128]{4,3,2,1,0:T(8,128)}) custom-call(bf16[8,32,1458]{2,1,0:T(8,128)(2,1)} %get-tuple-element.17.tf, bf16[1728,864]{1,0:T(8,128)(2,1)} %wd.1, bf16[1728,864]{1,0:T(8,128)(2,1)} %wx.1), custom_call_target="tpu_custom_call" | custom-call | flops 1337720832 | bytes 8000000 | tf_op jit(solution)/shard_map/ph/pallas_call | solution.py:195
  44.6 48.9 %ladder.1 = (f32[8,32,768]{2,1,0:T(8,128)}, f32[8,2,56,128]{3,2,1,0:T(8,128)}, f32[8,4,56,128]{3,2,1,0:T(8,128)}) custom-call(bf16[256,1458]{1,0:T(8,128)(2,1)} %bitcast.1, bf16[256,32]{1,0:T(8,128)(2,1)} %get-tuple-element.15.mt, bf16[32,5832]{1,0:T(8,128)(2,1)} %get-tuple-element.16.tb, f32[2,8,2,56,128]{4,3,2,1,0:T(8,128)} %get-tuple-element.18.so, ...), custom_call_target="tpu_custom_call" | custom-call | flops 4353564672 | bytes 20000000 | tf_op jit(solution)/shard_map/ladder/pallas_call | solution.py:336
  93.4 4.0 %final.1 = f32[32,5832]{1,0:T(8,128)} custom-call(f32[8,32,768]{2,1,0:T(8,128)} %get-tuple-element.20.rs, bf16[32,5832]{1,0:T(8,128)(2,1)} %v_ref.3, f32[32,5832]{1,0:T(8,128)} %d_ref.1, f32[2,8,2,56,128]{4,3,2,1,0:T(8,128)} %get-tuple-element.18.so, f32[8,2,56,128]{3,2,1,0:T(8,128)} %get-tuple-element.21.sz, f32[8,4,56,128]{3,2,1,0:T(8,128)} %get-tuple-element.22.strr), custom_call_target="tpu_custom_call" | custom-call | flops 1000000 | bytes 4000000 | tf_op jit(solution)/shard_map/final/pallas_call | solution.py:380
